TPU v7x, 32 devices: a whole 2x2x4 slice. The times are simulated.
32 devices in a mesh: gx: 4 (over y, core), gy: 2 (over x), ta: 4 (over z).
Axes of the slice: x: 2, y: 2, z: 4, core: 2. Of those that a mesh axis runs over, the one named last changes fastest.
Arguments:
- link_x: float32 [2, 3, 3, 16, 16, 256], P(None, None, None, 'gx', 'ta', 'gy'), may hold values from -1 to 1, as said below
- link_t: float32 [2, 3, 3, 16, 16, 256], P(None, None, None, 'gx', 'ta', 'gy'), may hold values from -1 to 1, as said below
Outputs:
- loops: float32 [6, 6, 16, 16], P(None, None, 'gx', 'ta')
Inputs may be any that keep to these rules, and one draw needn't show every extreme that they name: `link_x`: every link matrix is special unitary. `link_t`: every link matrix is special unitary.
All inputs are finite; a program needn't handle non-finite values.
Results may differ from a plain program's by a relative error of at most 0.0001.
Values sent between devices are 32-bit elements; how exact they have to be, the bound alone decides.
A program may use at most 128 MiB of HBM per device.

v0:
```python
import functools

import jax
import jax.numpy as jnp
from jax import lax
from jax.experimental import pallas as pl
from jax.experimental.pallas import tpu as pltpu
from jax.sharding import PartitionSpec as P

RMAX = 6
TMAX = 6
LANES = 128
ROWS = 8
MESH = pl.DeviceIdType.MESH


def product(left, right):
    (ar, ai), (br, bi) = left, right
    real = imag = None
    for j in range(3):
        a_re, a_im = ar[:, j][:, None], ai[:, j][:, None]
        b_re, b_im = br[j][None], bi[j][None]
        re = a_re * b_re - a_im * b_im
        im = a_re * b_im + a_im * b_re
        real = re if real is None else real + re
        imag = im if imag is None else imag + im
    return real, imag


def product_dagger(left, right):
    (ar, ai), (br, bi) = left, right
    real = imag = None
    for j in range(3):
        a_re, a_im = ar[:, j][:, None], ai[:, j][:, None]
        b_re, b_im = br[:, j][None], bi[:, j][None]
        re = a_re * b_re + a_im * b_im
        im = a_im * b_re - a_re * b_im
        real = re if real is None else real + re
        imag = im if imag is None else imag + im
    return real, imag


def load(ref, start):
    block = ref[:, pl.ds(start, ROWS), :]
    block = block.reshape(2, 3, 3, ROWS, LANES)
    return block[0], block[1]


def store(ref, start, mat):
    ref[0:9, pl.ds(start, ROWS), :] = mat[0].reshape(9, ROWS, LANES)
    ref[9:18, pl.ds(start, ROWS), :] = mat[1].reshape(9, ROWS, LANES)


def complete(two_rows):
    re = two_rows[0:6].reshape(2, 3, ROWS, LANES)
    im = two_rows[6:12].reshape(2, 3, ROWS, LANES)
    third_re, third_im = [], []
    for k in range(3):
        p, q = (k + 1) % 3, (k + 2) % 3
        third_re.append(
            re[0, p] * re[1, q] - im[0, p] * im[1, q] - re[0, q] * re[1, p] + im[0, q] * im[1, p]
        )
        third_im.append(
            re[0, q] * im[1, p] + im[0, q] * re[1, p] - re[0, p] * im[1, q] - im[0, p] * re[1, q]
        )
    real = jnp.concatenate([re, jnp.stack(third_re)[None]], axis=0)
    imag = jnp.concatenate([im, jnp.stack(third_im)[None]], axis=0)
    return real, imag


def kernel(
    dims, lx_ref, lt_ref, out_ref, raw, send, recv, links, pref, trans, part, gath,
    in_sem, own_sem, send_sem, recv_sem, send2_sem, recv2_sem,
):
    gx, gy, ta, nx, nt, ns, sub = dims
    groups = gx * ta
    total_t = ta * nt
    mx, my, mt = lax.axis_index("gx"), lax.axis_index("gy"), lax.axis_index("ta")
    me = mt * gx + mx
    comps = 24
    sites = nx * nt

    loads = []
    for f, ref in enumerate((lx_ref, lt_ref)):
        for c in range(2):
            q = f * 2 + c
            loads.append(
                pltpu.make_async_copy(
                    ref.at[c, pl.ds(0, 6 * sites)],
                    raw.at[pl.ds(q * 6 * sites, 6 * sites)],
                    in_sem.at[q],
                )
            )
            loads[-1].start()

    offsets = [(a, b, c) for c in range(ta) for b in range(gy) for a in range(gx)]
    offsets = [o for o in reversed(offsets) if o != (0, 0, 0)]

    def target(offset):
        a, b, c = offset
        return {
            "gx": lax.rem(mx + a, gx),
            "gy": lax.rem(my + b, gy),
            "ta": lax.rem(mt + c, ta),
        }

    barrier = pltpu.get_barrier_semaphore()
    for offset in offsets:
        pl.semaphore_signal(barrier, inc=1, device_id=target(offset), device_id_type=MESH)

    for copy in loads:
        copy.wait()
    width = nt * comps
    spare = LANES - width

    def layer(x):
        rows = [raw[pl.ds(x * nt + t, comps, stride=sites), :] for t in range(nt)]
        return jnp.concatenate(rows, axis=0)

    last = layer(nx - 1)
    for x in range(nx - 1):
        turned = jnp.concatenate([layer(x), last[x * spare : (x + 1) * spare]], axis=0).T
        send[:, pl.ds(x * sub, sub), :] = turned.reshape(groups, sub, LANES)

    pl.semaphore_wait(barrier, len(offsets))

    plane = [o for o in offsets if o[1] == 0]
    copies = []
    for k, offset in enumerate(plane):
        where = target(offset)
        copies.append(
            pltpu.make_async_remote_copy(
                src_ref=send.at[where["ta"] * gx + where["gx"]],
                dst_ref=recv.at[me],
                send_sem=send_sem.at[k],
                recv_sem=recv_sem.at[k],
                device_id=where,
                device_id_type=MESH,
            )
        )
        copies[-1].start()
    own = pltpu.make_async_copy(send.at[me], recv.at[me], own_sem.at[0])
    own.start()
    own.wait()

    lane_x = lax.broadcasted_iota(jnp.int32, (width, LANES), 1) // sub % nx
    for c in range(ta):
        for copy, offset in zip(copies, plane):
            if offset[2] == c:
                copy.wait()
        t_dev = lax.rem(mt + ta - c, ta)
        block = recv[pl.ds(t_dev * gx, gx)]
        block = jnp.concatenate([block, jnp.zeros((gx, sub, LANES), jnp.float32)], axis=1)
        block = block.reshape(LANES, LANES).T
        rest = [pltpu.roll(block[width:], (nx - 1 - x) * sub, 1) for x in range(nx - 1)]
        block = jnp.where(lane_x == nx - 1, jnp.concatenate(rest, axis=0), block[:width])
        for t in range(nt):
            links[:, t_dev * nt + t, :] = block[t * comps : (t + 1) * comps]

    for e in range(18):
        value = 1.0 if e in (0, 4, 8) else 0.0
        pref[e, 0:ROWS, :] = jnp.full((ROWS, LANES), value, jnp.float32)
    for start in range(0, total_t, ROWS):
        store(pref, ROWS + start, complete(links[12:24, pl.ds(start, ROWS), :]))
    step = 1
    while step < total_t:
        for start in reversed(range(0, total_t, ROWS)):
            if start + ROWS > step:
                earlier = load(pref, ROWS + start - step)
                store(pref, ROWS + start, product(earlier, load(pref, ROWS + start)))
        step *= 2
    loop = pref[:, total_t + ROWS - 1 : total_t + ROWS, :].reshape(2, 3, 3, 1, LANES)
    loop = jnp.broadcast_to(loop, (2, 3, 3, ROWS, LANES))
    store(pref, ROWS + total_t, product((loop[0], loop[1]), load(pref, ROWS)))

    def next_x(mat):
        return tuple(
            pltpu.roll(m.reshape(9 * ROWS, LANES), LANES - sub, 1).reshape(3, 3, ROWS, LANES)
            for m in mat
        )

    for start in range(0, total_t + ROWS, ROWS):
        gauge = load(pref, ROWS - 1 + start)
        link = complete(links[0:12, pl.ds(start % total_t, ROWS), :])
        moved = product_dagger(product(gauge, link), next_x(gauge))
        store(trans.at[0], start, moved)
        path = moved
        for r in range(1, RMAX):
            moved = next_x(moved)
            path = product(path, moved)
            store(trans.at[r], start, path)

    lane = lax.broadcasted_iota(jnp.int32, (total_t, LANES), 1)
    row = lax.broadcasted_iota(jnp.int32, (total_t, LANES), 0)
    sums = []
    for r in range(RMAX):
        for u in range(1, TMAX + 1):
            halves = []
            for start in range(0, total_t, ROWS):
                here = trans[r, :, pl.ds(start, ROWS), :]
                there = trans[r, :, pl.ds(start + u, ROWS), :]
                halves.append(jnp.sum(here * there, axis=0))
            sums.append(jnp.concatenate(halves, axis=0))

    def merge(items, width):
        if width == 0:
            return items[0]
        half = width
        low = [i for i in items[:half]]
        high = [i for i in items[half:]]
        first = merge(low, width // 2)
        first = first + pltpu.roll(first, LANES - width, 1)
        if not high:
            return first
        second = merge(high, width // 2)
        second = second + pltpu.roll(second, width, 1)
        return jnp.where((lane & width) == 0, first, second)

    def fold(items):
        return merge(items, sub // 2)

    block = LANES // gx
    for g in range(-(-len(sums) // sub)):
        value = fold(sums[g * sub : (g + 1) * sub])
        bit = 1
        while bit < gx:
            i_bit = (row & bit) != 0
            j_bit = ((lane // block) & bit) != 0
            up = pltpu.roll(pltpu.roll(value, total_t - bit, 0), block * bit, 1)
            down = pltpu.roll(pltpu.roll(value, bit, 0), LANES - block * bit, 1)
            value = jnp.where(i_bit == j_bit, value, jnp.where(j_bit, up, down))
            bit *= 2
        part[:, g, :] = value

    slot = my * groups + me
    copies2 = []
    for k, offset in enumerate(offsets):
        where = target(offset)
        copies2.append(
            pltpu.make_async_remote_copy(
                src_ref=part.at[where["ta"] * gx + where["gx"]],
                dst_ref=gath.at[slot],
                send_sem=send2_sem.at[k],
                recv_sem=recv2_sem.at[k],
                device_id=where,
                device_id_type=MESH,
            )
        )
        copies2[-1].start()
    own2 = pltpu.make_async_copy(part.at[me], gath.at[slot], own_sem.at[1])
    own2.start()
    own2.wait()
    for copy in copies2:
        copy.wait()
    out_ref[...] = jnp.sum(gath[...], axis=0) / (3.0 * (ns * gy))


def fast(dims, link_x, link_t):
    gx, gy, ta, nx, nt, ns, sub = dims
    groups = gx * ta
    total_t = ta * nt
    flat = (2, 9 * nx * nt, ns)
    rows = -(-RMAX * TMAX // sub)
    out = pl.pallas_call(
        functools.partial(kernel, dims),
        out_shape=jax.ShapeDtypeStruct((rows, LANES), jnp.float32),
        in_specs=[pl.BlockSpec(memory_space=pl.ANY)] * 2,
        out_specs=pl.BlockSpec(memory_space=pltpu.VMEM),
        scratch_shapes=[
            pltpu.VMEM((24 * nx * nt, ns), jnp.float32),
            pltpu.VMEM((groups, (nx - 1) * sub, LANES), jnp.float32),
            pltpu.VMEM((groups, (nx - 1) * sub, LANES), jnp.float32),
            pltpu.VMEM((24, total_t, LANES), jnp.float32),
            pltpu.VMEM((18, total_t + 2 * ROWS, LANES), jnp.float32),
            pltpu.VMEM((RMAX, 18, total_t + ROWS, LANES), jnp.float32),
            pltpu.VMEM((groups, rows, LANES), jnp.float32),
            pltpu.VMEM((gy * groups, rows, LANES), jnp.float32),
            pltpu.SemaphoreType.DMA((4,)),
            pltpu.SemaphoreType.DMA((2,)),
            pltpu.SemaphoreType.DMA((groups - 1,)),
            pltpu.SemaphoreType.DMA((groups - 1,)),
            pltpu.SemaphoreType.DMA((gy * groups - 1,)),
            pltpu.SemaphoreType.DMA((gy * groups - 1,)),
        ],
        compiler_params=pltpu.CompilerParams(collective_id=0, has_side_effects=True),
        name="wilson",
    )(link_x.reshape(flat), link_t.reshape(flat))
    loops = out.reshape(rows, nt, nx, sub).transpose(0, 3, 2, 1)
    return loops.reshape(rows * sub, nx, nt)[: RMAX * TMAX].reshape(RMAX, TMAX, nx, nt)


def times(left, right):
    def dot(a, b):
        return sum(a[:, j][:, None] * b[j][None] for j in range(3))

    real = dot(left[0], right[0]) - dot(left[1], right[1])
    imag = dot(left[0], right[1]) + dot(left[1], right[0])
    return jnp.stack([real, imag])


def general(dims, link_x, link_t):
    gx, gy, ta, nx, nt, ns, sub = dims

    def gather(field):
        field = lax.all_to_all(field, "gx", 5, 3, tiled=True)
        return lax.all_to_all(field, "ta", 5, 4, tiled=True)

    link_x, link_t = gather(link_x), gather(link_t)

    def grow_t(carry, _):
        line, factor = carry
        factor = jnp.roll(factor, -1, axis=4)
        return (times(line, factor), factor), line

    _, temporal = lax.scan(grow_t, (link_t, link_t), None, length=TMAX)

    def radius(carry, _):
        spatial, factor, carried = carry
        carried = jnp.roll(carried, -1, axis=4)

        def extent(shifted, pair):
            line, line_r = pair
            shifted = jnp.roll(shifted, -1, axis=4)
            return shifted, jnp.sum(times(spatial, line_r) * times(line, shifted), axis=(0, 1, 2, 5))

        _, sums = lax.scan(extent, spatial, (temporal, carried))
        factor = jnp.roll(factor, -1, axis=3)
        return (times(spatial, factor), factor, carried), sums

    _, loops = lax.scan(radius, (link_x, link_x, temporal), None, length=RMAX)
    loops = lax.psum(loops, ("gx", "gy", "ta"))
    loops = lax.dynamic_slice_in_dim(loops, lax.axis_index("gx") * nx, nx, axis=2)
    loops = lax.dynamic_slice_in_dim(loops, lax.axis_index("ta") * nt, nt, axis=3)
    return loops / (3.0 * (ns * gy))


def local(link_x, link_t):
    gx, gy, ta = (lax.axis_size(a) for a in ("gx", "gy", "ta"))
    nx, nt, ns = link_x.shape[3:]
    sub = ns // (gx * ta)
    dims = (gx, gy, ta, nx, nt, ns, sub)
    fits = (
        ns == LANES
        and sub == ROWS
        and gx * nx * sub == LANES
        and nt == gx
        and gx & (gx - 1) == 0
        and nt * 24 < LANES
        and nt * 24 == (nx - 1) * (LANES - nt * 24)
        and (ta * nt) % ROWS == 0
        and ta * nt >= TMAX
    )
    return (fast if fits else general)(dims, link_x, link_t)


def solution(mesh):
    spec = P(None, None, None, "gx", "ta", "gy")
    return jax.shard_map(
        local,
        mesh=mesh,
        in_specs=(spec, spec),
        out_specs=P(None, None, "gx", "ta"),
        check_vma=False,
    )
```

profile of v0, /device:TPU:0, one launch (start us, length us, event | category | flops | bytes accessed | tf_op | source)
XLA Modules:
  0.0 22.5 jit_solution(1823577420438546976)
XLA Ops:
  0.0 20.9 %wilson.1 = f32[5,128]{1,0:T(8,128)} custom-call(f32[2,144,128]{2,1,0:T(8,128)} %bitcast.11, f32[2,144,128]{2,1,0:T(8,128)} %bitcast.12), custom_call_target="tpu_custom_call" | custom-call | tf_op jit(solution)/shard_map/wilson/pallas_call | solution.py:264
  20.9 0.8 %reshape.17 = f32[5,4,4,8]{3,2,1,0:T(4,128)S(1)} reshape(f32[5,128]{1,0:T(8,128)} %wilson.1) | data formatting | bytes 5120 | tf_op jit(solution)/shard_map/reshape | solution.py:288
  21.7 0.1 reshape.18
  21.8 0.1 reshape.19
  21.9 0.6 %copy.4 = f32[6,6,4,4]{1,3,2,0:T(4,128)} copy(f32[6,6,4,4]{1,0,3,2:T(8,128)S(1)} %reshape.19) | data formatting | bytes 4608 | tf_op jit(solution)/shard_map/reshape | solution.py:289
  (1 shorter events, 0.0 us)
where the time goes:
time: 22.7 us; the launch traced here: 22.5 us
  Pallas kernels  20.9 us (92%)
  local copies, waits for them, and re-layouts  1.61 us (7%)
    pallas_call x1, Pallas kernels, fast(): pl.pallas_call(functools.partial(kernel, dims), out_shape=jax.ShapeDtypeS...  20.9 us
    reshape x3, local copies, waits for them, and re-layouts, fast(): loops.reshape(rows * sub, nx, nt)[:RMAX * TMAX].reshape(RMAX, TMAX, nx, nt)  0.81 us
    reshape x2, local copies, waits for them, and re-layouts, fast(): loops = out.reshape(rows, nt, nx, sub).transpose(0, 3, 2, 1)  0.8 us

commit v1 on v0

--- a/solution.py
+++ b/solution.py
@@ -66,6 +66,23 @@
     real = jnp.concatenate([re, jnp.stack(third_re)[None]], axis=0)
     imag = jnp.concatenate([im, jnp.stack(third_im)[None]], axis=0)
     return real, imag
+
+
+def spread(total, nx, nt, sub, out_ref):
+    shape = (nx * nt, LANES)
+    corner = lax.broadcasted_iota(jnp.int32, shape, 0)
+    column = lax.broadcasted_iota(jnp.int32, shape, 1)
+    base = (corner % nt) * (nx * sub) + (corner // nt) * sub
+    for r in range(RMAX):
+        first = r * TMAX // sub
+        item = jnp.minimum(column + (r * TMAX - first * sub), 2 * sub - 1)
+        lanes = base + item % sub
+        value = None
+        for g in range(first, (r * TMAX + TMAX - 1) // sub + 1):
+            line = jnp.broadcast_to(total[g : g + 1], shape)
+            line = jnp.take_along_axis(line, lanes, axis=1)
+            value = line if value is None else jnp.where(item < sub, value, line)
+        out_ref[r] = value.reshape(nx, nt, LANES)[:, :, :TMAX]
 
 
 def kernel(
@@ -252,7 +269,7 @@
     own2.wait()
     for copy in copies2:
         copy.wait()
-    out_ref[...] = jnp.sum(gath[...], axis=0) / (3.0 * (ns * gy))
+    spread(jnp.sum(gath[...], axis=0) / (3.0 * (ns * gy)), nx, nt, sub, out_ref)
 
 
 def fast(dims, link_x, link_t):
@@ -263,7 +280,7 @@
     rows = -(-RMAX * TMAX // sub)
     out = pl.pallas_call(
         functools.partial(kernel, dims),
-        out_shape=jax.ShapeDtypeStruct((rows, LANES), jnp.float32),
+        out_shape=pltpu.VMEM((RMAX, nx, nt, TMAX), jnp.float32),
         in_specs=[pl.BlockSpec(memory_space=pl.ANY)] * 2,
         out_specs=pl.BlockSpec(memory_space=pltpu.VMEM),
         scratch_shapes=[
@@ -285,8 +302,7 @@
         compiler_params=pltpu.CompilerParams(collective_id=0, has_side_effects=True),
         name="wilson",
     )(link_x.reshape(flat), link_t.reshape(flat))
-    loops = out.reshape(rows, nt, nx, sub).transpose(0, 3, 2, 1)
-    return loops.reshape(rows * sub, nx, nt)[: RMAX * TMAX].reshape(RMAX, TMAX, nx, nt)
+    return out.transpose(0, 3, 1, 2)
 
 
 def times(left, right):

time: 22.7 us -> 21.2 us (0.934)
  local copies, waits for them, and re-layouts: 1.61 us -> 0.62 us
  Pallas kernels: 20.9 us -> 20.4 us
    reshape x5 -> x0, local copies, waits for them, and re-layouts: 1.61 us -> none  [the longest x3 0.81 us: fast(): loops.reshape(rows * sub, nx, nt)[:RMAX * TMAX].reshape(RMAX, TMAX, nx, nt)]
    unnamed x0 -> x1, local copies, waits for them, and re-layouts: none -> 0.62 us
    pallas_call x1, Pallas kernels: 20.9 us -> 20.4 us  [fast(): pl.pallas_call(functools.partial(kernel, dims), out_shape=pltpu.VMEM((RMA...]
where the time goes in v1:
time: 21.2 us; the launch traced here: 21.1 us
  Pallas kernels  20.4 us (96%)
  local copies, waits for them, and re-layouts  0.62 us (3%)
    pallas_call x1, Pallas kernels, fast(): pl.pallas_call(functools.partial(kernel, dims), out_shape=pltpu.VMEM((RMA...  20.4 us
    unnamed x1, local copies, waits for them, and re-layouts  0.62 us

profile of v1, /device:TPU:0, one launch (start us, length us, event | category | flops | bytes accessed | tf_op | source)
XLA Modules:
  0.0 21.1 jit_solution(3917904726104363481)
XLA Ops:
  0.0 20.4 %wilson.1 = f32[6,4,4,6]{3,2,1,0:T(4,128)S(1)} custom-call(f32[2,144,128]{2,1,0:T(8,128)} %bitcast.4, f32[2,144,128]{2,1,0:T(8,128)} %bitcast.5), custom_call_target="tpu_custom_call" | custom-call | tf_op jit(solution)/shard_map/wilson/pallas_call | solution.py:281
  20.4 0.6 %copy.4 = f32[6,6,4,4]{1,3,2,0:T(4,128)} copy(f32[6,6,4,4]{1,3,2,0:T(4,128)S(1)} %bitcast.3) | data formatting | bytes 4608

commit v2 on v1

--- a/solution.py
+++ b/solution.py
@@ -87,7 +87,7 @@
 
 def kernel(
     dims, lx_ref, lt_ref, out_ref, raw, send, recv, links, pref, trans, part, gath,
-    in_sem, own_sem, send_sem, recv_sem, send2_sem, recv2_sem,
+    in_sem, send_sem, recv_sem, send2_sem, recv2_sem, entered,
 ):
     gx, gy, ta, nx, nt, ns, sub = dims
     groups = gx * ta
@@ -105,7 +105,7 @@
                 pltpu.make_async_copy(
                     ref.at[c, pl.ds(0, 6 * sites)],
                     raw.at[pl.ds(q * 6 * sites, 6 * sites)],
-                    in_sem.at[q],
+                    in_sem,
                 )
             )
             loads[-1].start()
@@ -121,12 +121,13 @@
             "ta": lax.rem(mt + c, ta),
         }
 
+    plane = [o for o in offsets if o[1] == 0]
+    peers = [o for o in offsets if o[0] == 0 and o[2] == 0]
     barrier = pltpu.get_barrier_semaphore()
-    for offset in offsets:
+    for offset in plane + peers:
         pl.semaphore_signal(barrier, inc=1, device_id=target(offset), device_id_type=MESH)
 
-    for copy in loads:
-        copy.wait()
+    pltpu.make_async_copy(raw, raw, in_sem).wait()
     width = nt * comps
     spare = LANES - width
 
@@ -139,9 +140,10 @@
         turned = jnp.concatenate([layer(x), last[x * spare : (x + 1) * spare]], axis=0).T
         send[:, pl.ds(x * sub, sub), :] = turned.reshape(groups, sub, LANES)
 
-    pl.semaphore_wait(barrier, len(offsets))
-
-    plane = [o for o in offsets if o[1] == 0]
+    pl.semaphore_wait(barrier, len(plane + peers))
+    for offset in peers:
+        pl.semaphore_signal(entered, inc=1, device_id=target(offset), device_id_type=MESH)
+
     copies = []
     for k, offset in enumerate(plane):
         where = target(offset)
@@ -149,22 +151,19 @@
             pltpu.make_async_remote_copy(
                 src_ref=send.at[where["ta"] * gx + where["gx"]],
                 dst_ref=recv.at[me],
-                send_sem=send_sem.at[k],
-                recv_sem=recv_sem.at[k],
+                send_sem=send_sem,
+                recv_sem=recv_sem.at[offset[2]],
                 device_id=where,
                 device_id_type=MESH,
             )
         )
         copies[-1].start()
-    own = pltpu.make_async_copy(send.at[me], recv.at[me], own_sem.at[0])
-    own.start()
-    own.wait()
+    recv[pl.ds(me, 1)] = send[pl.ds(me, 1)]
 
     lane_x = lax.broadcasted_iota(jnp.int32, (width, LANES), 1) // sub % nx
     for c in range(ta):
-        for copy, offset in zip(copies, plane):
-            if offset[2] == c:
-                copy.wait()
+        landed = recv.at[pl.ds(0, gx if c else gx - 1)]
+        pltpu.make_async_copy(landed, landed, recv_sem.at[c]).wait()
         t_dev = lax.rem(mt + ta - c, ta)
         block = recv[pl.ds(t_dev * gx, gx)]
         block = jnp.concatenate([block, jnp.zeros((gx, sub, LANES), jnp.float32)], axis=1)
@@ -250,6 +249,7 @@
         part[:, g, :] = value
 
     slot = my * groups + me
+    pl.semaphore_wait(entered, len(peers))
     copies2 = []
     for k, offset in enumerate(offsets):
         where = target(offset)
@@ -257,18 +257,19 @@
             pltpu.make_async_remote_copy(
                 src_ref=part.at[where["ta"] * gx + where["gx"]],
                 dst_ref=gath.at[slot],
-                send_sem=send2_sem.at[k],
-                recv_sem=recv2_sem.at[k],
+                send_sem=send2_sem,
+                recv_sem=recv2_sem,
                 device_id=where,
                 device_id_type=MESH,
             )
         )
         copies2[-1].start()
-    own2 = pltpu.make_async_copy(part.at[me], gath.at[slot], own_sem.at[1])
-    own2.start()
-    own2.wait()
-    for copy in copies2:
-        copy.wait()
+    gath[pl.ds(slot, 1)] = part[pl.ds(me, 1)]
+    sent = send.at[pl.ds(0, len(plane))]
+    pltpu.make_async_copy(sent, sent, send_sem).wait()
+    landed = gath.at[pl.ds(0, len(offsets))]
+    pltpu.make_async_copy(landed, landed, send2_sem).wait()
+    pltpu.make_async_copy(landed, landed, recv2_sem).wait()
     spread(jnp.sum(gath[...], axis=0) / (3.0 * (ns * gy)), nx, nt, sub, out_ref)
 
 
@@ -292,12 +293,12 @@
             pltpu.VMEM((RMAX, 18, total_t + ROWS, LANES), jnp.float32),
             pltpu.VMEM((groups, rows, LANES), jnp.float32),
             pltpu.VMEM((gy * groups, rows, LANES), jnp.float32),
-            pltpu.SemaphoreType.DMA((4,)),
-            pltpu.SemaphoreType.DMA((2,)),
-            pltpu.SemaphoreType.DMA((groups - 1,)),
-            pltpu.SemaphoreType.DMA((groups - 1,)),
-            pltpu.SemaphoreType.DMA((gy * groups - 1,)),
-            pltpu.SemaphoreType.DMA((gy * groups - 1,)),
+            pltpu.SemaphoreType.DMA,
+            pltpu.SemaphoreType.DMA,
+            pltpu.SemaphoreType.DMA((ta,)),
+            pltpu.SemaphoreType.DMA,
+            pltpu.SemaphoreType.DMA,
+            pltpu.SemaphoreType.REGULAR,
         ],
         compiler_params=pltpu.CompilerParams(collective_id=0, has_side_effects=True),
         name="wilson",

time: 21.2 us -> 20.3 us (0.958)
  Pallas kernels: 20.4 us -> 19.5 us
    pallas_call x1, Pallas kernels: 20.4 us -> 19.5 us  [fast(): pl.pallas_call(functools.partial(kernel, dims), out_shape=pltpu.VMEM((RMA...]
where the time goes in v2:
time: 20.3 us; the launch traced here: 20.1 us
  Pallas kernels  19.5 us (96%)
  local copies, waits for them, and re-layouts  0.62 us (3%)
    pallas_call x1, Pallas kernels, fast(): pl.pallas_call(functools.partial(kernel, dims), out_shape=pltpu.VMEM((RMA...  19.5 us
    unnamed x1, local copies, waits for them, and re-layouts  0.62 us

profile of v2, /device:TPU:0, one launch (start us, length us, event | category | flops | bytes accessed | tf_op | source)
XLA Modules:
  0.0 20.1 jit_solution(6888642548488201749)
XLA Ops:
  0.0 19.5 %wilson.1 = f32[6,4,4,6]{3,2,1,0:T(4,128)S(1)} custom-call(f32[2,144,128]{2,1,0:T(8,128)} %bitcast.4, f32[2,144,128]{2,1,0:T(8,128)} %bitcast.5), custom_call_target="tpu_custom_call" | custom-call | tf_op jit(solution)/shard_map/wilson/pallas_call | solution.py:282
  19.5 0.6 %copy.4 = f32[6,6,4,4]{1,3,2,0:T(4,128)} copy(f32[6,6,4,4]{1,3,2,0:T(4,128)S(1)} %bitcast.3) | data formatting | bytes 4608

commit v3 on v2

v3 whole, which is shorter than its diff:
```python
import contextlib
import functools

import jax
import jax.numpy as jnp
from jax import lax
from jax.experimental import pallas as pl
from jax.experimental.pallas import tpu as pltpu
from jax.sharding import PartitionSpec as P

RMAX = 6
TMAX = 6
LANES = 128
ROWS = 8
MESH = pl.DeviceIdType.MESH
scope = lambda name: contextlib.nullcontext()


def product(left, right):
    (ar, ai), (br, bi) = left, right
    real = imag = None
    for j in range(3):
        a_re, a_im = ar[:, j][:, None], ai[:, j][:, None]
        b_re, b_im = br[j][None], bi[j][None]
        re = a_re * b_re - a_im * b_im
        im = a_re * b_im + a_im * b_re
        real = re if real is None else real + re
        imag = im if imag is None else imag + im
    return real, imag


def product_dagger(left, right):
    (ar, ai), (br, bi) = left, right
    real = imag = None
    for j in range(3):
        a_re, a_im = ar[:, j][:, None], ai[:, j][:, None]
        b_re, b_im = br[:, j][None], bi[:, j][None]
        re = a_re * b_re + a_im * b_im
        im = a_im * b_re - a_re * b_im
        real = re if real is None else real + re
        imag = im if imag is None else imag + im
    return real, imag


def third(two):
    (ar, br), (ai, bi) = ((m[0], m[1]) for m in two)
    real, imag = [], []
    for k in range(3):
        p, q = (k + 1) % 3, (k + 2) % 3
        real.append(ar[p] * br[q] - ai[p] * bi[q] - ar[q] * br[p] + ai[q] * bi[p])
        imag.append(ar[q] * bi[p] + ai[q] * br[p] - ar[p] * bi[q] - ai[p] * br[q])
    return jnp.stack(real), jnp.stack(imag)


def full(two):
    return tuple(jnp.concatenate([m, t[None]], axis=0) for m, t in zip(two, third(two)))


def unit_where(mask, mat):
    rows = mat[0].shape[0]
    real = [
        jnp.stack([jnp.where(mask, mat[0][i, k], 1.0 if i == k else 0.0) for k in range(3)])
        for i in range(rows)
    ]
    return jnp.stack(real), jnp.where(mask, mat[1], 0.0)


def rolled(mat, shift, axis):
    return tuple(
        pltpu.roll(m.reshape(-1, *m.shape[2:]), shift, axis).reshape(m.shape) for m in mat
    )


def pivot(mat):
    size = [jnp.maximum(jnp.abs(mat[0][0, k]), jnp.abs(mat[1][0, k])) for k in range(3)]
    first = (size[0] >= size[1]) & (size[0] >= size[2])
    return first, size[1] >= size[2]


def choose(masks, a, b, c):
    return jnp.where(masks[0], a, jnp.where(masks[1], b, c))


def shorten(mat):
    masks = pivot(mat)
    parts = [m[0, k] for m in mat for k in range(3)]
    for m in mat:
        b = m[1]
        parts.append(choose(masks, b[1], b[2], b[0]))
        parts.append(choose(masks, b[2], b[0], b[1]))
    return parts


def lengthen(parts):
    ar, ai = parts[0:3], parts[3:6]
    (pr, qr), (pi, qi) = parts[6:8], parts[8:10]
    masks = pivot((parts[None, 0:3], parts[None, 3:6]))
    cr, ci = (choose(masks, a[0], a[1], a[2]) for a in (ar, ai))
    dr, di = (choose(masks, a[1], a[2], a[0]) for a in (ar, ai))
    er, ei = (choose(masks, a[2], a[0], a[1]) for a in (ar, ai))
    wr = dr * pr + di * pi + er * qr + ei * qi
    wi = dr * pi - di * pr + er * qi - ei * qr
    scale = -1.0 / (cr * cr + ci * ci)
    kr, ki = (wr * cr - wi * ci) * scale, (wr * ci + wi * cr) * scale
    second = []
    for k, p, q in ((kr, pr, qr), (ki, pi, qi)):
        second.append(jnp.stack([choose(masks, k, q, p), choose(masks, p, k, q), choose(masks, q, p, k)]))
    return jnp.stack([ar, second[0]]), jnp.stack([ai, second[1]])


def pair(block):
    half = block.reshape(2, -1, *block.shape[1:])
    return tuple(m.reshape(-1, 3, *block.shape[1:]) for m in half)


def flat(mat):
    return jnp.concatenate([m.reshape(-1, *m.shape[2:]) for m in mat], axis=0)


def swap(block, sub):
    row = lax.broadcasted_iota(jnp.int32, block.shape, 1) // (ROWS // 2)
    lane = lax.broadcasted_iota(jnp.int32, block.shape, 2) // sub % 2
    turned = pltpu.roll(block, ROWS // 2, 1)
    up, down = pltpu.roll(turned, sub, 2), pltpu.roll(turned, LANES - sub, 2)
    return jnp.where(row == lane, block, jnp.where(lane == 1, up, down))


def spread(total, nx, nt, sub, out_ref):
    shape = (nx * nt, LANES)
    corner = lax.broadcasted_iota(jnp.int32, shape, 0)
    column = lax.broadcasted_iota(jnp.int32, shape, 1)
    base = (corner % nt) * (nx * sub) + (corner // nt) * sub
    for r in range(RMAX):
        first = r * TMAX // sub
        item = jnp.minimum(column + (r * TMAX - first * sub), 2 * sub - 1)
        lanes = base + item % sub
        value = None
        for g in range(first, (r * TMAX + TMAX - 1) // sub + 1):
            line = jnp.broadcast_to(total[g : g + 1], shape)
            line = jnp.take_along_axis(line, lanes, axis=1)
            value = line if value is None else jnp.where(item < sub, value, line)
        out_ref[r] = value.reshape(nx, nt, LANES)[:, :, :TMAX]


def kernel(
    dims, lx_ref, lt_ref, out_ref, raw, first, block, send, recv, lines, edge, middle, step_t, trans, part,
    gath, in_sem, send_sem, recv_sem, send2_sem, recv2_sem, entered,
):
    gx, gy, ta, nx, nt, ns, sub = dims
    groups = gx * ta
    total_t = ta * nt
    mx, my, mt = lax.axis_index("gx"), lax.axis_index("gy"), lax.axis_index("ta")
    me = mt * gx + mx
    sites = nx * nt
    comps = 12
    short = 10

    offsets = [(a, b, c) for c in range(ta) for b in range(gy) for a in range(gx)]
    offsets = [o for o in reversed(offsets) if o != (0, 0, 0)]
    plane = [o for o in offsets if o[1] == 0]
    peers = [o for o in offsets if o[0] == 0 and o[2] == 0]

    def target(offset):
        a, b, c = offset
        return {
            "gx": lax.rem(mx + a, gx),
            "gy": lax.rem(my + b, gy),
            "ta": lax.rem(mt + c, ta),
        }

    barrier = pltpu.get_barrier_semaphore()
    for offset in plane + peers:
        pl.semaphore_signal(barrier, inc=1, device_id=target(offset), device_id_type=MESH)

    for f, ref in enumerate((lt_ref, lx_ref)):
        for c in range(2):
            pltpu.make_async_copy(
                ref.at[c, pl.ds(0, 6 * sites)],
                raw.at[f, pl.ds(c * 6 * sites, 6 * sites)],
                in_sem.at[f],
            ).start()

    with scope("p_load"):
        pltpu.make_async_copy(raw.at[0], raw.at[0], in_sem.at[0]).wait()
    with scope("p_local"):
        t_local = lax.broadcasted_iota(jnp.int32, (sites, LANES), 0) % nt
        x_local = lax.broadcasted_iota(jnp.int32, (sites, LANES), 0) // nt
        line = pair(raw[0].reshape(comps, sites, LANES))
        step = 1
        while step < nt:
            earlier = unit_where(t_local >= step, rolled(line, step, 1))
            line = product(earlier, full(line))
            step *= 2
        first[...] = flat(line).reshape(comps * sites, LANES)
        for k in range(2):
            for m in range(3):
                for xl in range(2):
                    block[k, pl.ds(short * ROWS + m * ROWS + xl * 4, 4), :] = first[
                        pl.ds(4 * m * sites + (2 * k + xl) * nt + nt - 1, 4, stride=sites), :
                    ]
            for tt in range(2):
                block[k, pl.ds(short * ROWS + 2 * comps + tt * comps, comps), :] = first[
                    pl.ds(2 * k + tt, comps, stride=sites), :
                ]
        gauge = unit_where(t_local >= 1, rolled(line, 1, 1))
        pltpu.make_async_copy(raw.at[1], raw.at[1], in_sem.at[1]).wait()
        link = full(pair(raw[1].reshape(comps, sites, LANES)))
        beyond = unit_where(x_local < nx - 1, rolled(full(gauge), sites - nt, 1))
        parts = shorten(product_dagger(product(gauge, link), beyond))
        for k in range(2):
            for c in range(short):
                block[k, pl.ds(c * ROWS, ROWS), :] = parts[c][k * ROWS : (k + 1) * ROWS]
            send[:, pl.ds(k * sub, sub), :] = block[k].T.reshape(groups, sub, LANES)

    with scope("p_bar"):
        pl.semaphore_wait(barrier, len(plane + peers))
    for offset in peers:
        pl.semaphore_signal(entered, inc=1, device_id=target(offset), device_id_type=MESH)

    for k, offset in enumerate(plane):
        where = target(offset)
        pltpu.make_async_remote_copy(
            src_ref=send.at[where["ta"] * gx + where["gx"]],
            dst_ref=recv.at[me],
            send_sem=send_sem,
            recv_sem=recv_sem.at[mt // 2],
            device_id=where,
            device_id_type=MESH,
        ).start()
    own = pltpu.make_async_copy(send.at[me], recv.at[me], recv_sem.at[mt // 2])
    own.start()

    def next_x(mat):
        return tuple(
            pltpu.roll(m.reshape(-1, LANES), LANES - sub, 1).reshape(m.shape) for m in mat
        )

    t_half = lax.broadcasted_iota(jnp.int32, (ROWS, LANES), 0) % nt
    x_lane = lax.broadcasted_iota(jnp.int32, (ROWS, LANES), 1) // sub % nx
    for order in range(2):
        half = lax.rem(mt // 2 + order, 2)
        landed = recv.at[pl.ds(half * 2 * gx, 2 * gx)]
        with scope(f"p_w{order}"):
            pltpu.make_async_copy(landed, landed, recv_sem.at[half]).wait()
        with scope(f"p_half{order}"):
            got = recv[pl.ds(half * 2 * gx, 2 * gx)].reshape(2, gx, 2, sub, LANES)
            got = jnp.stack([jnp.stack([got[0, a, k], got[1, a, k]]) for a in range(gx) for k in range(2)])
            got = got.reshape(LANES, LANES).T
            parts = swap(got[: short * ROWS].reshape(short, ROWS, LANES), sub)
            ends = swap(got[short * ROWS : short * ROWS + 2 * comps].reshape(3, ROWS, LANES), sub)
            for m in range(3):
                for td in range(2):
                    lines[pl.ds(4 * m * ROWS + half * 2 + td + 1, 4, stride=ROWS), :] = ends[m, td * 4 : td * 4 + 4]
            starts = got[short * ROWS + 2 * comps :]
            for td in range(2):
                near = pltpu.roll(starts, LANES - sub * (1 + td), 1)
                far = pltpu.roll(starts, LANES - sub * (3 + td), 1)
                edge[pl.ds(td * nt + 1, comps, stride=ROWS), :] = near[:comps]
                edge[pl.ds(td * nt + 2, comps, stride=ROWS), :] = near[comps:]
                edge[pl.ds(td * nt + 3, comps, stride=ROWS), :] = far[:comps]
            end = pair(edge[...].reshape(comps, ROWS, LANES))
            end = full(unit_where((t_half > 0) & (x_lane == nx - 1), end))
            middle[:, pl.ds(half * ROWS, ROWS), :] = flat(product_dagger(lengthen(parts), end))

    with scope("p_prefix"):
        row = lax.broadcasted_iota(jnp.int32, (ROWS, LANES), 0)
        hop = lines[...].reshape(comps, ROWS, LANES)
        hop = jnp.where(row == ta + 1, pltpu.roll(hop, ta, 1), hop)
        hop = unit_where((row > 0) & (row < ta + 2), pair(hop))
        step = 1
        while step < ta + 2:
            earlier = unit_where(row >= step, rolled(hop, step, 1))
            hop = product(earlier, full(hop))
            step *= 2
        hop = full(hop)
        step_t[0] = flat(hop).reshape(18 * ROWS, LANES)
        step_t[1] = flat(next_x(hop)).reshape(18 * ROWS, LANES)

    def spread_t(side, rows, v):
        out = []
        for c in range(18):
            if c % 9 >= 3 * rows:
                continue
            low, high = (
                jnp.broadcast_to(step_t[side, pl.ds(c * ROWS + 2 * v + td, 1), :], (ROWS, LANES))
                for td in range(2)
            )
            out.append(jnp.where(row < nt, low, high))
        return pair(jnp.stack(out))

    with scope("p_path"):
        for v in range(total_t // ROWS + 1):
            start = v * ROWS
            inner = pair(middle[:, pl.ds(start % total_t, ROWS), :])
            moved = product(spread_t(0, 2, v), full(product_dagger(inner, spread_t(1, 3, v))))
            path = moved
            moved = full(moved)
            trans[0, :, pl.ds(start, ROWS), :] = flat(moved)
            for r in range(1, RMAX):
                moved = next_x(moved)
                path = product(path, moved)
                trans[r, :, pl.ds(start, ROWS), :] = flat(full(path))

    lane = lax.broadcasted_iota(jnp.int32, (total_t, LANES), 1)
    row = lax.broadcasted_iota(jnp.int32, (total_t, LANES), 0)
    sums = []
    with scope("p_sums"):
        for r in range(RMAX):
            for u in range(1, TMAX + 1):
                halves = []
                for start in range(0, total_t, ROWS):
                    here = trans[r, :, pl.ds(start, ROWS), :]
                    there = trans[r, :, pl.ds(start + u, ROWS), :]
                    halves.append(jnp.sum(here * there, axis=0))
                sums.append(jnp.concatenate(halves, axis=0))

    def merge(items, width):
        if width == 0:
            return items[0]
        half = width
        low = [i for i in items[:half]]
        high = [i for i in items[half:]]
        first = merge(low, width // 2)
        first = first + pltpu.roll(first, LANES - width, 1)
        if not high:
            return first
        second = merge(high, width // 2)
        second = second + pltpu.roll(second, width, 1)
        return jnp.where((lane & width) == 0, first, second)

    def fold(items):
        return merge(items, sub // 2)

    block = LANES // gx
    with scope("p_fold"):
        for g in range(-(-len(sums) // sub)):
            value = fold(sums[g * sub : (g + 1) * sub])
            bit = 1
            while bit < gx:
                i_bit = (row & bit) != 0
                j_bit = ((lane // block) & bit) != 0
                up = pltpu.roll(pltpu.roll(value, total_t - bit, 0), block * bit, 1)
                down = pltpu.roll(pltpu.roll(value, bit, 0), LANES - block * bit, 1)
                value = jnp.where(i_bit == j_bit, value, jnp.where(j_bit, up, down))
                bit *= 2
            part[:, g, :] = value

    slot = my * groups + me
    pl.semaphore_wait(entered, len(peers))
    copies2 = []
    for k, offset in enumerate(offsets):
        where = target(offset)
        copies2.append(
            pltpu.make_async_remote_copy(
                src_ref=part.at[where["ta"] * gx + where["gx"]],
                dst_ref=gath.at[slot],
                send_sem=send2_sem,
                recv_sem=recv2_sem,
                device_id=where,
                device_id_type=MESH,
            )
        )
        copies2[-1].start()
    gath[pl.ds(slot, 1)] = part[pl.ds(me, 1)]
    with scope("p_wait2"):
        sent = send.at[pl.ds(0, len(plane))]
        pltpu.make_async_copy(sent, sent, send_sem).wait()
        landed = gath.at[pl.ds(0, len(offsets))]
        pltpu.make_async_copy(landed, landed, send2_sem).wait()
        pltpu.make_async_copy(landed, landed, recv2_sem).wait()
    spread(jnp.sum(gath[...], axis=0) / (3.0 * (ns * gy)), nx, nt, sub, out_ref)


def fast(dims, link_x, link_t):
    gx, gy, ta, nx, nt, ns, sub = dims
    groups = gx * ta
    total_t = ta * nt
    flat = (2, 9 * nx * nt, ns)
    rows = -(-RMAX * TMAX // sub)
    out = pl.pallas_call(
        functools.partial(kernel, dims),
        out_shape=pltpu.VMEM((RMAX, nx, nt, TMAX), jnp.float32),
        in_specs=[pl.BlockSpec(memory_space=pl.ANY)] * 2,
        out_specs=pl.BlockSpec(memory_space=pltpu.VMEM),
        scratch_shapes=[
            pltpu.VMEM((2, 12 * nx * nt, ns), jnp.float32),
            pltpu.VMEM((12 * nx * nt, ns), jnp.float32),
            pltpu.VMEM((2, LANES, ns), jnp.float32),
            pltpu.VMEM((groups, 2 * sub, LANES), jnp.float32),
            pltpu.VMEM((groups, 2 * sub, LANES), jnp.float32),
            pltpu.VMEM((12 * ROWS, LANES), jnp.float32),
            pltpu.VMEM((12 * ROWS, LANES), jnp.float32),
            pltpu.VMEM((12, total_t, LANES), jnp.float32),
            pltpu.VMEM((2, 18 * ROWS, LANES), jnp.float32),
            pltpu.VMEM((RMAX, 18, total_t + ROWS, LANES), jnp.float32),
            pltpu.VMEM((groups, rows, LANES), jnp.float32),
            pltpu.VMEM((gy * groups, rows, LANES), jnp.float32),
            pltpu.SemaphoreType.DMA((2,)),
            pltpu.SemaphoreType.DMA,
            pltpu.SemaphoreType.DMA((2,)),
            pltpu.SemaphoreType.DMA,
            pltpu.SemaphoreType.DMA,
            pltpu.SemaphoreType.REGULAR,
        ],
        compiler_params=pltpu.CompilerParams(collective_id=0, has_side_effects=True),
        name="wilson",
    )(link_x.reshape(flat), link_t.reshape(flat))
    return out.transpose(0, 3, 1, 2)


def times(left, right):
    def dot(a, b):
        return sum(a[:, j][:, None] * b[j][None] for j in range(3))

    real = dot(left[0], right[0]) - dot(left[1], right[1])
    imag = dot(left[0], right[1]) + dot(left[1], right[0])
    return jnp.stack([real, imag])


def general(dims, link_x, link_t):
    gx, gy, ta, nx, nt, ns, sub = dims

    def gather(field):
        field = lax.all_to_all(field, "gx", 5, 3, tiled=True)
        return lax.all_to_all(field, "ta", 5, 4, tiled=True)

    link_x, link_t = gather(link_x), gather(link_t)

    def grow_t(carry, _):
        line, factor = carry
        factor = jnp.roll(factor, -1, axis=4)
        return (times(line, factor), factor), line

    _, temporal = lax.scan(grow_t, (link_t, link_t), None, length=TMAX)

    def radius(carry, _):
        spatial, factor, carried = carry
        carried = jnp.roll(carried, -1, axis=4)

        def extent(shifted, pair):
            line, line_r = pair
            shifted = jnp.roll(shifted, -1, axis=4)
            return shifted, jnp.sum(times(spatial, line_r) * times(line, shifted), axis=(0, 1, 2, 5))

        _, sums = lax.scan(extent, spatial, (temporal, carried))
        factor = jnp.roll(factor, -1, axis=3)
        return (times(spatial, factor), factor, carried), sums

    _, loops = lax.scan(radius, (link_x, link_x, temporal), None, length=RMAX)
    loops = lax.psum(loops, ("gx", "gy", "ta"))
    loops = lax.dynamic_slice_in_dim(loops, lax.axis_index("gx") * nx, nx, axis=2)
    loops = lax.dynamic_slice_in_dim(loops, lax.axis_index("ta") * nt, nt, axis=3)
    return loops / (3.0 * (ns * gy))


def local(link_x, link_t):
    gx, gy, ta = (lax.axis_size(a) for a in ("gx", "gy", "ta"))
    nx, nt, ns = link_x.shape[3:]
    sub = ns // (gx * ta)
    dims = (gx, gy, ta, nx, nt, ns, sub)
    fits = (
        ns == LANES
        and sub == ROWS
        and gx == nx == nt == ta == 4
    )
    return (fast if fits else general)(dims, link_x, link_t)


def solution(mesh):
    spec = P(None, None, None, "gx", "ta", "gy")
    return jax.shard_map(
        local,
        mesh=mesh,
        in_specs=(spec, spec),
        out_specs=P(None, None, "gx", "ta"),
        check_vma=False,
    )
```

time: 20.3 us -> 18.4 us (0.906)
  Pallas kernels: 19.5 us -> 17.6 us
    pallas_call x1, Pallas kernels: 19.5 us -> 17.6 us  [fast(): pl.pallas_call(functools.partial(kernel, dims), out_shape=pltpu.VMEM((RMA...]
where the time goes in v3:
time: 18.4 us; the launch traced here: 18.3 us
  Pallas kernels  17.6 us (96%)
  local copies, waits for them, and re-layouts  0.62 us (3%)
    pallas_call x1, Pallas kernels, fast(): pl.pallas_call(functools.partial(kernel, dims), out_shape=pltpu.VMEM((RMA...  17.6 us
    unnamed x1, local copies, waits for them, and re-layouts  0.62 us

profile of v3, /device:TPU:0, one launch (start us, length us, event | category | flops | bytes accessed | tf_op | source)
XLA Modules:
  0.0 18.3 jit_solution(16076382424774748684)
XLA Ops:
  0.0 17.6 %wilson.1 = f32[6,4,4,6]{3,2,1,0:T(4,128)S(1)} custom-call(f32[2,144,128]{2,1,0:T(8,128)} %bitcast.4, f32[2,144,128]{2,1,0:T(8,128)} %bitcast.5), custom_call_target="tpu_custom_call" | custom-call | tf_op jit(solution)/shard_map/wilson/pallas_call | solution.py:380
  17.6 0.6 %copy.4 = f32[6,6,4,4]{1,3,2,0:T(4,128)} copy(f32[6,6,4,4]{1,3,2,0:T(4,128)S(1)} %bitcast.3) | data formatting | bytes 4608

commit v4 on v3

--- a/solution.py
+++ b/solution.py
@@ -117,23 +117,24 @@
     return jnp.concatenate([m.reshape(-1, *m.shape[2:]) for m in mat], axis=0)
 
 
-def swap(block, sub):
-    row = lax.broadcasted_iota(jnp.int32, block.shape, 1) // (ROWS // 2)
-    lane = lax.broadcasted_iota(jnp.int32, block.shape, 2) // sub % 2
-    turned = pltpu.roll(block, ROWS // 2, 1)
-    up, down = pltpu.roll(turned, sub, 2), pltpu.roll(turned, LANES - sub, 2)
-    return jnp.where(row == lane, block, jnp.where(lane == 1, up, down))
+def join(early, late, sub):
+    row = lax.broadcasted_iota(jnp.int32, early.shape, 1) // (ROWS // 2)
+    lane = lax.broadcasted_iota(jnp.int32, early.shape, 2) // sub % 2
+    early_turned, late_turned = (pltpu.roll(b, ROWS // 2, 1) for b in (early, late))
+    even = jnp.where(row == 0, early, late_turned)
+    odd = jnp.where(row == 0, early_turned, late)
+    return jnp.where(lane == 0, even, odd)
 
 
 def spread(total, nx, nt, sub, out_ref):
     shape = (nx * nt, LANES)
     corner = lax.broadcasted_iota(jnp.int32, shape, 0)
     column = lax.broadcasted_iota(jnp.int32, shape, 1)
-    base = (corner % nt) * (nx * sub) + (corner // nt) * sub
+    base = (corner // nt) * (sub * nt) + corner % nt
     for r in range(RMAX):
         first = r * TMAX // sub
         item = jnp.minimum(column + (r * TMAX - first * sub), 2 * sub - 1)
-        lanes = base + item % sub
+        lanes = base + item % sub * nt
         value = None
         for g in range(first, (r * TMAX + TMAX - 1) // sub + 1):
             line = jnp.broadcast_to(total[g : g + 1], shape)
@@ -243,18 +244,17 @@
         with scope(f"p_w{order}"):
             pltpu.make_async_copy(landed, landed, recv_sem.at[half]).wait()
         with scope(f"p_half{order}"):
-            got = recv[pl.ds(half * 2 * gx, 2 * gx)].reshape(2, gx, 2, sub, LANES)
-            got = jnp.stack([jnp.stack([got[0, a, k], got[1, a, k]]) for a in range(gx) for k in range(2)])
-            got = got.reshape(LANES, LANES).T
-            parts = swap(got[: short * ROWS].reshape(short, ROWS, LANES), sub)
-            ends = swap(got[short * ROWS : short * ROWS + 2 * comps].reshape(3, ROWS, LANES), sub)
+            got = recv[pl.ds(half * 2 * gx, 2 * gx)].reshape(2, gx * 2, sub, LANES)
+            got = [jnp.stack([got[td], got[td]], axis=1).reshape(LANES, LANES).T for td in range(2)]
+            cuts = short * ROWS, short * ROWS + 2 * comps
+            parts = join(*(g[: cuts[0]].reshape(short, ROWS, LANES) for g in got), sub)
+            ends = join(*(g[cuts[0] : cuts[1]].reshape(3, ROWS, LANES) for g in got), sub)
             for m in range(3):
                 for td in range(2):
                     lines[pl.ds(4 * m * ROWS + half * 2 + td + 1, 4, stride=ROWS), :] = ends[m, td * 4 : td * 4 + 4]
-            starts = got[short * ROWS + 2 * comps :]
             for td in range(2):
-                near = pltpu.roll(starts, LANES - sub * (1 + td), 1)
-                far = pltpu.roll(starts, LANES - sub * (3 + td), 1)
+                near = pltpu.roll(got[td][cuts[1] :], LANES - sub, 1)
+                far = pltpu.roll(got[td][cuts[1] : cuts[1] + 2 * ROWS], LANES - 3 * sub, 1)
                 edge[pl.ds(td * nt + 1, comps, stride=ROWS), :] = near[:comps]
                 edge[pl.ds(td * nt + 2, comps, stride=ROWS), :] = near[comps:]
                 edge[pl.ds(td * nt + 3, comps, stride=ROWS), :] = far[:comps]
@@ -288,62 +288,63 @@
             out.append(jnp.where(row < nt, low, high))
         return pair(jnp.stack(out))
 
+    row_t = row // nt
+    lane = lax.broadcasted_iota(jnp.int32, (ROWS, LANES), 1)
+    block_x = lane // (LANES // nx)
+    own_time = row % nt * (LANES // nx) + lane % (LANES // nx)
+
+    def emit(items, g, held):
+        stack = []
+        for td in range(ta):
+            for a, b in zip(items[::2], items[1::2]):
+                a, b = a[td // 2], b[td // 2]
+                if td % 2:
+                    stack.append(jnp.where(row_t == 0, pltpu.roll(a, nt, 0), b))
+                else:
+                    stack.append(jnp.where(row_t == 0, a, pltpu.roll(b, nt, 0)))
+            stack += [jnp.zeros((ROWS, LANES), jnp.float32)] * ((sub - len(items)) // 2)
+        turned = jnp.concatenate(stack, axis=0).T.reshape(gx * nx, sub, LANES)
+        for step in (4, 2, 1):
+            turned = turned + pltpu.roll(turned, step, 1)
+        if g % 2 == 0 and g < rows - 1:
+            return turned
+        low = turned if held is None else held
+        for j in range(gx):
+            value = None
+            for x in range(nx):
+                both = jnp.where(row_t == 0, low[j * nx + x], turned[j * nx + x])
+                both = jnp.take_along_axis(both, own_time, axis=1)
+                value = both if value is None else jnp.where(block_x == x, both, value)
+            for k in range(1 if held is None else 2):
+                part[pl.ds(j * ROWS + g // 2 * 2 + k, ta, stride=gx * ROWS), :] = value[k * nt : k * nt + ta]
+        return None
+
+    rows = -(-RMAX * TMAX // sub)
     with scope("p_path"):
         for v in range(total_t // ROWS + 1):
             start = v * ROWS
             inner = pair(middle[:, pl.ds(start % total_t, ROWS), :])
             moved = product(spread_t(0, 2, v), full(product_dagger(inner, spread_t(1, 3, v))))
-            path = moved
-            moved = full(moved)
-            trans[0, :, pl.ds(start, ROWS), :] = flat(moved)
-            for r in range(1, RMAX):
-                moved = next_x(moved)
-                path = product(path, moved)
-                trans[r, :, pl.ds(start, ROWS), :] = flat(full(path))
-
-    lane = lax.broadcasted_iota(jnp.int32, (total_t, LANES), 1)
-    row = lax.broadcasted_iota(jnp.int32, (total_t, LANES), 0)
-    sums = []
+            trans[0, :, pl.ds(start, ROWS), :] = flat(full(moved))
     with scope("p_sums"):
+        items, g, held = [], 0, None
         for r in range(RMAX):
+            for v in range(total_t // ROWS + 1) if r else ():
+                here = pl.ds(v * ROWS, ROWS)
+                moved = pair(pltpu.roll(trans[0, :, here, :].reshape(-1, LANES), LANES - r * sub, 1).reshape(18, ROWS, LANES))
+                path = pair(trans[r - 1, :, here, :])
+                path = product((path[0][:2], path[1][:2]), moved)
+                trans[r, :, here, :] = flat(full(path))
             for u in range(1, TMAX + 1):
-                halves = []
-                for start in range(0, total_t, ROWS):
-                    here = trans[r, :, pl.ds(start, ROWS), :]
-                    there = trans[r, :, pl.ds(start + u, ROWS), :]
-                    halves.append(jnp.sum(here * there, axis=0))
-                sums.append(jnp.concatenate(halves, axis=0))
-
-    def merge(items, width):
-        if width == 0:
-            return items[0]
-        half = width
-        low = [i for i in items[:half]]
-        high = [i for i in items[half:]]
-        first = merge(low, width // 2)
-        first = first + pltpu.roll(first, LANES - width, 1)
-        if not high:
-            return first
-        second = merge(high, width // 2)
-        second = second + pltpu.roll(second, width, 1)
-        return jnp.where((lane & width) == 0, first, second)
-
-    def fold(items):
-        return merge(items, sub // 2)
-
-    block = LANES // gx
-    with scope("p_fold"):
-        for g in range(-(-len(sums) // sub)):
-            value = fold(sums[g * sub : (g + 1) * sub])
-            bit = 1
-            while bit < gx:
-                i_bit = (row & bit) != 0
-                j_bit = ((lane // block) & bit) != 0
-                up = pltpu.roll(pltpu.roll(value, total_t - bit, 0), block * bit, 1)
-                down = pltpu.roll(pltpu.roll(value, bit, 0), LANES - block * bit, 1)
-                value = jnp.where(i_bit == j_bit, value, jnp.where(j_bit, up, down))
-                bit *= 2
-            part[:, g, :] = value
+                items.append(
+                    [
+                        jnp.sum(trans[r, :, pl.ds(start, ROWS), :] * trans[r, :, pl.ds(start + u, ROWS), :], axis=0)
+                        for start in range(0, total_t, ROWS)
+                    ]
+                )
+                if len(items) == sub or (r, u) == (RMAX - 1, TMAX):
+                    held = emit(items, g, held)
+                    items, g = [], g + 1
 
     slot = my * groups + me
     pl.semaphore_wait(entered, len(peers))
@@ -352,7 +353,7 @@
         where = target(offset)
         copies2.append(
             pltpu.make_async_remote_copy(
-                src_ref=part.at[where["ta"] * gx + where["gx"]],
+                src_ref=part.at[pl.ds((where["ta"] * gx + where["gx"]) * ROWS, rows)],
                 dst_ref=gath.at[slot],
                 send_sem=send2_sem,
                 recv_sem=recv2_sem,
@@ -361,7 +362,7 @@
             )
         )
         copies2[-1].start()
-    gath[pl.ds(slot, 1)] = part[pl.ds(me, 1)]
+    gath[slot] = part[pl.ds(me * ROWS, rows), :]
     with scope("p_wait2"):
         sent = send.at[pl.ds(0, len(plane))]
         pltpu.make_async_copy(sent, sent, send_sem).wait()
@@ -393,7 +394,7 @@
             pltpu.VMEM((12, total_t, LANES), jnp.float32),
             pltpu.VMEM((2, 18 * ROWS, LANES), jnp.float32),
             pltpu.VMEM((RMAX, 18, total_t + ROWS, LANES), jnp.float32),
-            pltpu.VMEM((groups, rows, LANES), jnp.float32),
+            pltpu.VMEM((groups * ROWS, LANES), jnp.float32),
             pltpu.VMEM((gy * groups, rows, LANES), jnp.float32),
             pltpu.SemaphoreType.DMA((2,)),
             pltpu.SemaphoreType.DMA,

time: 18.4 us -> 18.1 us (0.984)
  Pallas kernels: 17.6 us -> 17.3 us
    pallas_call x1, Pallas kernels: 17.6 us -> 17.3 us  [fast(): pl.pallas_call(functools.partial(kernel, dims), out_shape=pltpu.VMEM((RMA...]
where the time goes in v4:
time: 18.1 us; the launch traced here: 17.9 us
  Pallas kernels  17.3 us (96%)
  local copies, waits for them, and re-layouts  0.62 us (3%)
    pallas_call x1, Pallas kernels, fast(): pl.pallas_call(functools.partial(kernel, dims), out_shape=pltpu.VMEM((RMA...  17.3 us
    unnamed x1, local copies, waits for them, and re-layouts  0.62 us

profile of v4, /device:TPU:0, one launch (start us, length us, event | category | flops | bytes accessed | tf_op | source)
XLA Modules:
  0.0 17.9 jit_solution(16759406985704424758)
XLA Ops:
  0.0 17.3 %wilson.1 = f32[6,4,4,6]{3,2,1,0:T(4,128)S(1)} custom-call(f32[2,144,128]{2,1,0:T(8,128)} %bitcast.4, f32[2,144,128]{2,1,0:T(8,128)} %bitcast.5), custom_call_target="tpu_custom_call" | custom-call | tf_op jit(solution)/shard_map/wilson/pallas_call | solution.py:381
  17.3 0.6 %copy.4 = f32[6,6,4,4]{1,3,2,0:T(4,128)} copy(f32[6,6,4,4]{1,3,2,0:T(4,128)S(1)} %bitcast.3) | data formatting | bytes 4608

commit v5 on v4

--- a/solution.py
+++ b/solution.py
@@ -156,22 +156,24 @@
     comps = 12
     short = 10
 
-    offsets = [(a, b, c) for c in range(ta) for b in range(gy) for a in range(gx)]
-    offsets = [o for o in reversed(offsets) if o != (0, 0, 0)]
-    plane = [o for o in offsets if o[1] == 0]
-    peers = [o for o in offsets if o[0] == 0 and o[2] == 0]
-
-    def target(offset):
-        a, b, c = offset
+    steps = [(a, b, c, d) for a in range(2) for b in range(2) for c in range(gy) for d in range(ta)]
+    steps = [o for o in steps if any(o)]
+    plane = [o for o in steps if o[2] == 0]
+    plane.sort(key=lambda o: (-o[3], -o[0], o[1]))
+    steps.sort(key=lambda o: (-o[2], -min(o[3], ta - o[3]) - o[0], o[1], o[3]))
+    peers = [o for o in steps if o[0] == o[1] == o[3] == 0]
+
+    def target(step):
+        a, b, c, d = step
         return {
-            "gx": lax.rem(mx + a, gx),
-            "gy": lax.rem(my + b, gy),
-            "ta": lax.rem(mt + c, ta),
+            "gx": lax.rem(mx // 2 + a, 2) * 2 + lax.rem(mx + b, 2),
+            "gy": lax.rem(my + c, gy),
+            "ta": lax.rem(mt + d, ta),
         }
 
     barrier = pltpu.get_barrier_semaphore()
-    for offset in plane + peers:
-        pl.semaphore_signal(barrier, inc=1, device_id=target(offset), device_id_type=MESH)
+    for step in plane + peers:
+        pl.semaphore_signal(barrier, inc=1, device_id=target(step), device_id_type=MESH)
 
     for f, ref in enumerate((lt_ref, lx_ref)):
         for c in range(2):
@@ -215,11 +217,11 @@
 
     with scope("p_bar"):
         pl.semaphore_wait(barrier, len(plane + peers))
-    for offset in peers:
-        pl.semaphore_signal(entered, inc=1, device_id=target(offset), device_id_type=MESH)
-
-    for k, offset in enumerate(plane):
-        where = target(offset)
+    for step in peers:
+        pl.semaphore_signal(entered, inc=1, device_id=target(step), device_id_type=MESH)
+
+    for step in plane:
+        where = target(step)
         pltpu.make_async_remote_copy(
             src_ref=send.at[where["ta"] * gx + where["gx"]],
             dst_ref=recv.at[me],
@@ -347,11 +349,11 @@
                     items, g = [], g + 1
 
     slot = my * groups + me
-    pl.semaphore_wait(entered, len(peers))
-    copies2 = []
-    for k, offset in enumerate(offsets):
-        where = target(offset)
-        copies2.append(
+    with scope("p_entered"):
+        pl.semaphore_wait(entered, len(peers))
+    with scope("p_send2"):
+        for step in steps:
+            where = target(step)
             pltpu.make_async_remote_copy(
                 src_ref=part.at[pl.ds((where["ta"] * gx + where["gx"]) * ROWS, rows)],
                 dst_ref=gath.at[slot],
@@ -359,14 +361,12 @@
                 recv_sem=recv2_sem,
                 device_id=where,
                 device_id_type=MESH,
-            )
-        )
-        copies2[-1].start()
+            ).start()
     gath[slot] = part[pl.ds(me * ROWS, rows), :]
     with scope("p_wait2"):
         sent = send.at[pl.ds(0, len(plane))]
         pltpu.make_async_copy(sent, sent, send_sem).wait()
-        landed = gath.at[pl.ds(0, len(offsets))]
+        landed = gath.at[pl.ds(0, len(steps))]
         pltpu.make_async_copy(landed, landed, send2_sem).wait()
         pltpu.make_async_copy(landed, landed, recv2_sem).wait()
     spread(jnp.sum(gath[...], axis=0) / (3.0 * (ns * gy)), nx, nt, sub, out_ref)

time: 18.1 us -> 17.5 us (0.967)
  Pallas kernels: 17.3 us -> 16.7 us
    pallas_call x1, Pallas kernels: 17.3 us -> 16.7 us  [fast(): pl.pallas_call(functools.partial(kernel, dims), out_shape=pltpu.VMEM((RMA...]
where the time goes in v5:
time: 17.5 us; the launch traced here: 17.4 us
  Pallas kernels  16.7 us (95%)
  local copies, waits for them, and re-layouts  0.62 us (4%)
    pallas_call x1, Pallas kernels, fast(): pl.pallas_call(functools.partial(kernel, dims), out_shape=pltpu.VMEM((RMA...  16.7 us
    unnamed x1, local copies, waits for them, and re-layouts  0.62 us

profile of v5, /device:TPU:0, one launch (start us, length us, event | category | flops | bytes accessed | tf_op | source)
XLA Modules:
  0.0 17.4 jit_solution(16416727590784081180)
XLA Ops:
  0.0 16.7 %wilson.1 = f32[6,4,4,6]{3,2,1,0:T(4,128)S(1)} custom-call(f32[2,144,128]{2,1,0:T(8,128)} %bitcast.4, f32[2,144,128]{2,1,0:T(8,128)} %bitcast.5), custom_call_target="tpu_custom_call" | custom-call | tf_op jit(solution)/shard_map/wilson/pallas_call | solution.py:381
  16.7 0.6 %copy.4 = f32[6,6,4,4]{1,3,2,0:T(4,128)} copy(f32[6,6,4,4]{1,3,2,0:T(4,128)S(1)} %bitcast.3) | data formatting | bytes 4608

commit v6 on v5

--- a/solution.py
+++ b/solution.py
@@ -156,11 +156,19 @@
     comps = 12
     short = 10
 
+    inner = lax.rem((mt + 1) // 2, 2)
+    opposite, second = ta - 1 - mt, lax.rem(mt + 2, ta)
+    ranks = [
+        mt,
+        mt + 1 - 2 * lax.rem(mt, 2),
+        inner * opposite + (1 - inner) * second,
+        inner * second + (1 - inner) * opposite,
+    ]
     steps = [(a, b, c, d) for a in range(2) for b in range(2) for c in range(gy) for d in range(ta)]
     steps = [o for o in steps if any(o)]
     plane = [o for o in steps if o[2] == 0]
-    plane.sort(key=lambda o: (-o[3], -o[0], o[1]))
-    steps.sort(key=lambda o: (-o[2], -min(o[3], ta - o[3]) - o[0], o[1], o[3]))
+    plane.sort(key=lambda o: (-o[3] * 2 - o[0] * 3, o[1]))
+    steps.sort(key=lambda o: (-o[2] - o[0] - o[3], o[1]))
     peers = [o for o in steps if o[0] == o[1] == o[3] == 0]
 
     def target(step):
@@ -168,7 +176,7 @@
         return {
             "gx": lax.rem(mx // 2 + a, 2) * 2 + lax.rem(mx + b, 2),
             "gy": lax.rem(my + c, gy),
-            "ta": lax.rem(mt + d, ta),
+            "ta": ranks[d],
         }
 
     barrier = pltpu.get_barrier_semaphore()
@@ -176,12 +184,7 @@
         pl.semaphore_signal(barrier, inc=1, device_id=target(step), device_id_type=MESH)
 
     for f, ref in enumerate((lt_ref, lx_ref)):
-        for c in range(2):
-            pltpu.make_async_copy(
-                ref.at[c, pl.ds(0, 6 * sites)],
-                raw.at[f, pl.ds(c * 6 * sites, 6 * sites)],
-                in_sem.at[f],
-            ).start()
+        pltpu.make_async_copy(ref.at[:, pl.ds(0, 6 * sites)], raw.at[f], in_sem.at[f]).start()
 
     with scope("p_load"):
         pltpu.make_async_copy(raw.at[0], raw.at[0], in_sem.at[0]).wait()
@@ -384,7 +387,7 @@
         in_specs=[pl.BlockSpec(memory_space=pl.ANY)] * 2,
         out_specs=pl.BlockSpec(memory_space=pltpu.VMEM),
         scratch_shapes=[
-            pltpu.VMEM((2, 12 * nx * nt, ns), jnp.float32),
+            pltpu.VMEM((2, 2, 6 * nx * nt, ns), jnp.float32),
             pltpu.VMEM((12 * nx * nt, ns), jnp.float32),
             pltpu.VMEM((2, LANES, ns), jnp.float32),
             pltpu.VMEM((groups, 2 * sub, LANES), jnp.float32),

time: 17.5 us -> 17.4 us (level)
  no operation moved by 1% of the time
where the time goes in v6:
time: 17.4 us; the launch traced here: 17.2 us
  Pallas kernels  16.6 us (95%)
  local copies, waits for them, and re-layouts  0.62 us (4%)
    pallas_call x1, Pallas kernels, fast(): pl.pallas_call(functools.partial(kernel, dims), out_shape=pltpu.VMEM((RMA...  16.6 us
    unnamed x1, local copies, waits for them, and re-layouts  0.62 us

profile of v6, /device:TPU:0, one launch (start us, length us, event | category | flops | bytes accessed | tf_op | source)
XLA Modules:
  0.0 17.2 jit_solution(9096757124835209507)
XLA Ops:
  0.0 16.6 %wilson.1 = f32[6,4,4,6]{3,2,1,0:T(4,128)S(1)} custom-call(f32[2,144,128]{2,1,0:T(8,128)} %bitcast.4, f32[2,144,128]{2,1,0:T(8,128)} %bitcast.5), custom_call_target="tpu_custom_call" | custom-call | tf_op jit(solution)/shard_map/wilson/pallas_call | solution.py:384
  16.6 0.6 %copy.4 = f32[6,6,4,4]{1,3,2,0:T(4,128)} copy(f32[6,6,4,4]{1,3,2,0:T(4,128)S(1)} %bitcast.3) | data formatting | bytes 4608

commit v7 on v6

--- a/solution.py
+++ b/solution.py
@@ -184,7 +184,10 @@
         pl.semaphore_signal(barrier, inc=1, device_id=target(step), device_id_type=MESH)
 
     for f, ref in enumerate((lt_ref, lx_ref)):
-        pltpu.make_async_copy(ref.at[:, pl.ds(0, 6 * sites)], raw.at[f], in_sem.at[f]).start()
+        for c in range(2):
+            pltpu.make_async_copy(
+                ref.at[c, pl.ds(0, 6 * sites)], raw.at[f, pl.ds(c * 6 * sites, 6 * sites)], in_sem.at[f]
+            ).start()
 
     with scope("p_load"):
         pltpu.make_async_copy(raw.at[0], raw.at[0], in_sem.at[0]).wait()
@@ -372,7 +375,10 @@
         landed = gath.at[pl.ds(0, len(steps))]
         pltpu.make_async_copy(landed, landed, send2_sem).wait()
         pltpu.make_async_copy(landed, landed, recv2_sem).wait()
-    spread(jnp.sum(gath[...], axis=0) / (3.0 * (ns * gy)), nx, nt, sub, out_ref)
+    total = [gath[k] for k in range(gy * groups)]
+    while len(total) > 1:
+        total = [sum(total[k : k + 2]) for k in range(0, len(total), 2)]
+    spread(total[0] * (1.0 / (3.0 * (ns * gy))), nx, nt, sub, out_ref)
 
 
 def fast(dims, link_x, link_t):
@@ -387,7 +393,7 @@
         in_specs=[pl.BlockSpec(memory_space=pl.ANY)] * 2,
         out_specs=pl.BlockSpec(memory_space=pltpu.VMEM),
         scratch_shapes=[
-            pltpu.VMEM((2, 2, 6 * nx * nt, ns), jnp.float32),
+            pltpu.VMEM((2, 12 * nx * nt, ns), jnp.float32),
             pltpu.VMEM((12 * nx * nt, ns), jnp.float32),
             pltpu.VMEM((2, LANES, ns), jnp.float32),
             pltpu.VMEM((groups, 2 * sub, LANES), jnp.float32),

time: 17.4 us -> 17.4 us (level)
  no operation moved by 1% of the time
where the time goes in v7:
time: 17.4 us; the launch traced here: 17.2 us
  Pallas kernels  16.6 us (95%)
  local copies, waits for them, and re-layouts  0.62 us (4%)
    pallas_call x1, Pallas kernels, fast(): pl.pallas_call(functools.partial(kernel, dims), out_shape=pltpu.VMEM((RMA...  16.6 us
    unnamed x1, local copies, waits for them, and re-layouts  0.62 us

profile of v7, /device:TPU:0, one launch (start us, length us, event | category | flops | bytes accessed | tf_op | source)
XLA Modules:
  0.0 17.2 jit_solution(12639478406110504819)
XLA Ops:
  0.0 16.6 %wilson.1 = f32[6,4,4,6]{3,2,1,0:T(4,128)S(1)} custom-call(f32[2,144,128]{2,1,0:T(8,128)} %bitcast.4, f32[2,144,128]{2,1,0:T(8,128)} %bitcast.5), custom_call_target="tpu_custom_call" | custom-call | tf_op jit(solution)/shard_map/wilson/pallas_call | solution.py:390
  16.6 0.6 %copy.4 = f32[6,6,4,4]{1,3,2,0:T(4,128)} copy(f32[6,6,4,4]{1,3,2,0:T(4,128)S(1)} %bitcast.3) | data formatting | bytes 4608

commit v8 on v7

--- a/solution.py
+++ b/solution.py
@@ -312,8 +312,7 @@
                     stack.append(jnp.where(row_t == 0, a, pltpu.roll(b, nt, 0)))
             stack += [jnp.zeros((ROWS, LANES), jnp.float32)] * ((sub - len(items)) // 2)
         turned = jnp.concatenate(stack, axis=0).T.reshape(gx * nx, sub, LANES)
-        for step in (4, 2, 1):
-            turned = turned + pltpu.roll(turned, step, 1)
+        turned = turned + pltpu.roll(turned, nt, 1)
         if g % 2 == 0 and g < rows - 1:
             return turned
         low = turned if held is None else held
@@ -321,6 +320,8 @@
             value = None
             for x in range(nx):
                 both = jnp.where(row_t == 0, low[j * nx + x], turned[j * nx + x])
+                for swapped in (row + 2 - row // 2 % 2 * 4, row + 1 - row % 2 * 2):
+                    both = both + jnp.take_along_axis(both, swapped, axis=0)
                 both = jnp.take_along_axis(both, own_time, axis=1)
                 value = both if value is None else jnp.where(block_x == x, both, value)
             for k in range(1 if held is None else 2):

time: 17.4 us -> 17.4 us (level)
  no operation moved by 1% of the time
where the time goes in v8:
time: 17.4 us; the launch traced here: 17.2 us
  Pallas kernels  16.6 us (95%)
  local copies, waits for them, and re-layouts  0.62 us (4%)
    pallas_call x1, Pallas kernels, fast(): pl.pallas_call(functools.partial(kernel, dims), out_shape=pltpu.VMEM((RMA...  16.6 us
    unnamed x1, local copies, waits for them, and re-layouts  0.62 us

profile of v8, /device:TPU:0, one launch (start us, length us, event | category | flops | bytes accessed | tf_op | source)
XLA Modules:
  0.0 17.2 jit_solution(842766446827034332)
XLA Ops:
  0.0 16.6 %wilson.1 = f32[6,4,4,6]{3,2,1,0:T(4,128)S(1)} custom-call(f32[2,144,128]{2,1,0:T(8,128)} %bitcast.4, f32[2,144,128]{2,1,0:T(8,128)} %bitcast.5), custom_call_target="tpu_custom_call" | custom-call | tf_op jit(solution)/shard_map/wilson/pallas_call | solution.py:391
  16.6 0.6 %copy.4 = f32[6,6,4,4]{1,3,2,0:T(4,128)} copy(f32[6,6,4,4]{1,3,2,0:T(4,128)S(1)} %bitcast.3) | data formatting | bytes 4608
